TPU v7x, 32 devices: a whole 2x2x4 slice. The times are simulated.
32 devices in a mesh: gx: 4 (over y, core), gy: 8 (over z, x).
Axes of the slice: x: 2, y: 2, z: 4, core: 2. Of those that a mesh axis runs over, the one named last changes fastest.
Arguments:
- right_side: float32 [128, 256, 512], P('gx', 'gy'), as said below
- start_guess: float32 [128, 256, 512], P('gx', 'gy'), may hold values from -3 to 3
- conductivity: float32 [128, 256, 512], P('gx', 'gy'), may hold values from 0.5 to 8
Outputs:
- solution_field: float32 [128, 256, 512], P('gx', 'gy')
- estimate: float32 [], replicated
Inputs may be any that keep to these rules, and one draw needn't show every extreme that they name: `right_side`: A smoothly varying positive scale times noise, which may have a nonzero mean.
All inputs are finite; a program needn't handle non-finite values.
Results may differ from a plain program's by a relative error of at most 0.0003.
Values sent between devices are 32-bit elements; how exact they have to be, the bound alone decides.
No kernel may reach another device: no remote copies, remote signals or barrier semaphores. Data moves between devices by JAX's collectives and lax.ppermute only.
A program may use at most 64 MiB of HBM per device.

v0:
```python
import jax
import jax.numpy as jnp
from jax import lax
from jax.sharding import PartitionSpec as P

M = 3


def with_halo(cells, sides, width):
    for axis, dim in sides:
        count = lax.axis_size(axis)
        ends = count - 1
        head = lax.slice_in_dim(cells, 0, width, axis=dim)
        tail = lax.slice_in_dim(cells, cells.shape[dim] - width, cells.shape[dim], axis=dim)
        cells = jnp.concatenate(
            [
                lax.ppermute(tail, axis, [(i, (i + 1) % count) for i in range(ends)]),
                cells,
                lax.ppermute(head, axis, [((i + 1) % count, i) for i in range(ends)]),
            ],
            axis=dim,
        )
    return cells


def shifted(padded, which, sign):
    starts = [1, 1, 1]
    starts[which] = 1 + sign
    limits = [starts[dim] + padded.shape[dim] - 2 for dim in range(3)]
    return lax.slice(padded, starts, limits)


def extend_z(padded):
    return jnp.pad(padded, ((0, 0), (0, 0), (1, 1)))


def stencil(field, kappa_pad):
    padded = extend_z(with_halo(field, (("gx", 0), ("gy", 1)), 1))
    centre = shifted(padded, 0, 0)
    middle = shifted(kappa_pad, 0, 0)
    result = jnp.zeros_like(centre)
    for which in range(3):
        for sign in (-1, 1):
            result = result + 0.5 * (middle + shifted(kappa_pad, which, sign)) * (
                centre - shifted(padded, which, sign)
            )
    return result


def global_norm(vector):
    return jnp.sqrt(lax.psum(jnp.sum(vector * vector), ("gx", "gy")))


def least_squares(columns, beta):
    count = len(columns)
    rhs_vals = [beta] + [jnp.float32(0.0)] * count
    cosines = []
    sines = []
    upper = []
    for column in range(count):
        entries = list(columns[column])
        for earlier in range(column):
            first = entries[earlier]
            second = entries[earlier + 1]
            entries[earlier] = cosines[earlier] * first + sines[earlier] * second
            entries[earlier + 1] = -sines[earlier] * first + cosines[earlier] * second
        first = entries[column]
        second = entries[column + 1]
        radius = jnp.sqrt(first * first + second * second)
        cosines.append(first / radius)
        sines.append(second / radius)
        entries[column] = radius
        rhs_vals[column + 1] = -sines[column] * rhs_vals[column]
        rhs_vals[column] = cosines[column] * rhs_vals[column]
        upper.append(entries[: column + 1])
    coeffs = [None] * count
    for row in reversed(range(count)):
        value = rhs_vals[row]
        for later in range(row + 1, count):
            value = value - upper[later][row] * coeffs[later]
        coeffs[row] = value / upper[row][row]
    return (coeffs, jnp.abs(rhs_vals[count]))


def local(right_side, start_guess, conductivity):
    kappa_pad = extend_z(with_halo(conductivity, (("gx", 0), ("gy", 1)), 1))
    start = right_side - stencil(start_guess, kappa_pad)
    beta = global_norm(start)
    basis = [start / beta]
    columns = []
    for column in range(M):
        vector = stencil(basis[column], kappa_pad)
        local_dots = jnp.stack([jnp.sum(vector * basis[earlier]) for earlier in range(column + 1)])
        coeff_all, squares = lax.psum((local_dots, jnp.sum(vector * vector)), ("gx", "gy"))
        for earlier in range(column + 1):
            vector = vector - coeff_all[earlier] * basis[earlier]
        entries = [coeff_all[earlier] for earlier in range(column + 1)]
        length = jnp.sqrt(squares - jnp.sum(coeff_all * coeff_all))
        entries.append(length)
        columns.append(entries)
        basis.append(vector / length)
    coeffs, estimate = least_squares(columns, beta)
    solution_field = start_guess
    for column in range(M):
        solution_field = solution_field + coeffs[column] * basis[column]
    return (solution_field, estimate)


def solution(mesh):
    in_specs = (P("gx", "gy", None), P("gx", "gy", None), P("gx", "gy", None))
    out_specs = (P("gx", "gy", None), P())
    return jax.shard_map(local, mesh=mesh, in_specs=in_specs, out_specs=out_specs, check_vma=False)
```

profile of v0, /device:TPU:0, one launch (start us, length us, event | category | flops | bytes accessed | tf_op | source)
XLA Modules:
  0.0 344.9 jit_solution(8450779061837298228)
XLA Ops:
  1.6 2.4 collective-permute-start
  6.3 5.2 %collective-permute-start.1 = (f32[1,32,512]{2,0,1:T(1,128)S(1)}, f32[1,32,512]{2,0,1:T(1,128)S(1)}, u32[]{:S(2)}, u32[]{:S(2)}) collective-permute-start(f32[1,32,512]{2,0,1:T(1,128)S(1)} %copy.8), channel_id=1, source_target_pairs={{0,8},{8,16},{16,24},{1,9},{9,17},{17,25},{2,10},{10,18},{18,26},{... | collective-permute-start | bytes 196616 | tf_op jit(solution)/shard_map/ppermute | solution.py:17
  13.0 2.8 copy.7
  17.1 3.4 collective-permute-start.4
  21.9 4.6 %collective-permute-start.5 = (f32[34,1,512]{2,0,1:T(8,128)S(1)}, f32[34,1,512]{2,0,1:T(8,128)S(1)}, u32[]{:S(2)}, u32[]{:S(2)}) collective-permute-start(f32[34,1,512]{2,0,1:T(8,128)S(1)} %get-tuple-element.31), channel_id=1, source_target_pairs={{0,1},{1,2},{2,3},{3,4},{4,5},{5,6},{6,7},{8,9},{9,10},{10,11},{11... | collective-permute-start | bytes 208904 | tf_op jit(solution)/shard_map/ppermute | solution.py:17
  27.8 3.1 select_maximum_fusion.16
  30.9 2.4 collective-permute-done.7
  33.3 3.0 select_maximum_fusion.12
  36.4 9.9 %multiply_reduce_fusion.9 = (f32[]{:T(128)}, f32[32,32,512]{2,0,1:T(8,128)}) fusion(f32[32,32,512]{2,0,1:T(8,128)S(1)} %copy.28, f32[34,34,514]{2,0,1:T(8,128)S(1)} %select_maximum_fusion.12, f32[32,32,512]{2,0,1:T(8,128)S(1)} %copy.7, f32[34,34,514]{2,0,1:T(8,128)S(1)} %select_maximum_fusion.16, f32[34,1,512]{2,0,1:T(8,128)S(1)} %collective-permute-done.7, ...), kind=kLoop, calls=%fused_computation.156 | loop fusion | flops 25165824 | bytes 17317892 | tf_op jit(solution)/shard_map/reduce_sum | solution.py:51
  46.3 44.5 %psum.49 = f32[]{:T(128)} all-reduce(f32[]{:T(128)} %get-tuple-element.21), channel_id=1, replica_groups=mesh['gx'=4,'gy'=8] {'gx','gy'}, use_global_device_ids=true, to_apply=%region_1.2 | all-reduce | flops 1 | bytes 8 | tf_op jit(solution)/shard_map/psum | solution.py:51
  96.0 4.5 %collective-permute-done.9 = f32[1,32,512]{2,0,1:T(1,128)S(1)} collective-permute-done((f32[1,32,512]{2,0,1:T(1,128)S(1)}, f32[1,32,512]{2,0,1:T(1,128)S(1)}, u32[]{:S(2)}, u32[]{:S(2)}) %collective-permute-start.9) | collective-permute-done | bytes 65568 | tf_op jit(solution)/shard_map/ppermute | solution.py:19
  100.6 2.0 collective-permute-start.10
  104.7 4.5 %collective-permute-done.11 = f32[34,1,512]{2,0,1:T(8,128)S(1)} collective-permute-done((f32[34,1,512]{2,0,1:T(8,128)S(1)}, f32[34,1,512]{2,0,1:T(8,128)S(1)}, u32[]{:S(2)}, u32[]{:S(2)}) %collective-permute-start.11) | collective-permute-done | bytes 69664 | tf_op jit(solution)/shard_map/ppermute | solution.py:19
  109.1 3.0 select_maximum_fusion.8
  112.2 8.3 %multiply_reduce_fusion.8 = (f32[]{:T(128)}, f32[]{:T(128)}, f32[32,32,512]{2,0,1:T(8,128)}) fusion(f32[32,32,512]{2,0,1:T(8,128)S(1)} %broadcast_divide_fusion, f32[34,34,514]{2,0,1:T(8,128)S(1)} %select_maximum_fusion.8, f32[32,32,512]{2,0,1:T(8,128)S(1)} %copy-done.5, f32[34,34,514]{2,0,1:T(8,128)S(1)} %select_maximum_fusion.16, ...), kind=kLoop, calls=%fused_computation.155 | loop fusion | flops 25690112 | bytes 15220744 | tf_op jit(solution)/shard_map/reduce_sum | solution.py:93
  120.5 42.9 %all-reduce.7 = (f32[]{:T(128)}, f32[1]{0:T(128)}) all-reduce(f32[]{:T(128)} %get-tuple-element.12, f32[1]{0:T(128)} %bitcast), channel_id=1, replica_groups=mesh['gx'=4,'gy'=8] {'gx','gy'}, use_global_device_ids=true, to_apply=%region_5.6 | all-reduce | flops 2 | bytes 16 | tf_op jit(solution)/shard_map/psum | solution.py:94
  165.4 3.4 subtract_divide_fusion.1
  171.5 4.6 %collective-permute-done.13 = f32[1,32,512]{2,0,1:T(1,128)S(1)} collective-permute-done((f32[1,32,512]{2,0,1:T(1,128)S(1)}, f32[1,32,512]{2,0,1:T(1,128)S(1)}, u32[]{:S(2)}, u32[]{:S(2)}) %collective-permute-start.13) | collective-permute-done | bytes 65568 | tf_op jit(solution)/shard_map/ppermute | solution.py:19
  176.2 2.0 collective-permute-start.14
  180.2 4.6 %collective-permute-done.15 = f32[34,1,512]{2,0,1:T(8,128)S(1)} collective-permute-done((f32[34,1,512]{2,0,1:T(8,128)S(1)}, f32[34,1,512]{2,0,1:T(8,128)S(1)}, u32[]{:S(2)}, u32[]{:S(2)}) %collective-permute-start.15) | collective-permute-done | bytes 69664 | tf_op jit(solution)/shard_map/ppermute | solution.py:19
  184.8 3.0 select_maximum_fusion.4
  187.9 8.6 %multiply_reduce_fusion.6 = (f32[]{:T(128)}, f32[]{:T(128)}, f32[]{:T(128)}, f32[32,32,512]{2,0,1:T(8,128)}) fusion(f32[32,32,512]{2,0,1:T(8,128)S(1)} %subtract_divide_fusion.1, f32[34,34,514]{2,0,1:T(8,128)S(1)} %select_maximum_fusion.4, f32[32,32,512]{2,0,1:T(8,128)S(1)} %copy-done.6, f32[34,34,514]{2,0,1:T(8,128)S(1)} %select_maximum_fusion.16, ...), kind=kLoop, calls=%fused_computation.152 | loop fusion | flops 27262976 | bytes 17317904 | tf_op jit(solution)/shard_map/reduce_sum | solution.py:93
  197.9 42.9 %all-reduce.6 = (f32[]{:T(128)}, f32[2]{0:T(128)S(1)}) all-reduce(f32[]{:T(128)} %get-tuple-element.9, f32[2]{0:T(128)S(1)} %pad_maximum_fusion.55), channel_id=1, replica_groups=mesh['gx'=4,'gy'=8] {'gx','gy'}, use_global_device_ids=true, to_apply=%region_10.11 | all-reduce | flops 3 | bytes 24 | tf_op jit(solution)/shard_map/psum | solution.py:94
  243.6 5.0 %subtract_divide_fusion = f32[32,32,512]{2,0,1:T(8,128)S(1)} fusion(f32[32,32,512]{2,0,1:T(8,128)} %copy-done, f32[32,32,512]{2,0,1:T(8,128)} %get-tuple-element.19, f32[]{:T(128)S(6)} %sqrt.24, f32[]{:T(128)} %bitcast.6, f32[]{:T(128)} %bitcast.5, f32[32,32,512]{2,0,1:T(8,128)} %get-tuple-element.22, f32[]{:T(128)S(6)} %sqrt.21), kind=kLoop, calls=%fused_computation.149 | loop fusion | flops 3145728 | bytes 8388624 | tf_op jit(solution)/shard_map/div | solution.py:101
  251.3 4.6 %collective-permute-done.17 = f32[1,32,512]{2,0,1:T(1,128)S(1)} collective-permute-done((f32[1,32,512]{2,0,1:T(1,128)S(1)}, f32[1,32,512]{2,0,1:T(1,128)S(1)}, u32[]{:S(2)}, u32[]{:S(2)}) %collective-permute-start.17) | collective-permute-done | bytes 65568 | tf_op jit(solution)/shard_map/ppermute | solution.py:19
  256.6 2.6 collective-permute-start.18
  265.9 4.6 %select_maximum_fusion = f32[34,34,514]{2,0,1:T(8,128)S(1)} fusion(f32[34,1,512]{2,0,1:T(8,128)} %collective-permute-done.19, f32[34,1,512]{2,0,1:T(8,128)} %collective-permute-done.18, f32[1,32,512]{2,0,1:T(1,128)} %copy-done.24, f32[32,32,512]{2,0,1:T(8,128)} %copy-done.7, f32[1,32,512]{2,0,1:T(1,128)} %copy-done.22), kind=kLoop, calls=%fused_computation.2 | loop fusion | flops 7130208 | bytes 4744224 | tf_op jit(solution)/shard_map/concatenate | solution.py:15
  270.5 14.5 %multiply_reduce_fusion = (f32[]{:T(128)}, f32[]{:T(128)}, f32[]{:T(128)}, f32[]{:T(128)}) fusion(f32[32,32,512]{2,0,1:T(8,128)} %copy-done.7, f32[32,32,512]{2,0,1:T(8,128)S(1)} %copy-done.1, f32[34,34,514]{2,0,1:T(8,128)S(1)} %select_maximum_fusion, f32[32,32,512]{2,0,1:T(8,128)} %copy-done.4, f32[34,34,514]{2,0,1:T(8,128)S(1)} %select_maximum_fusion.16, ...), kind=kLoop, calls=%fused_computation.145 | loop fusion | flops 28311552 | bytes 17317908 | tf_op jit(solution)/shard_map/reduce_sum | solution.py:94
  285.0 1.9 pad_maximum_fusion.56
  286.9 42.5 %all-reduce.5 = (f32[3]{0:T(128)S(1)}, f32[]{:T(128)}) all-reduce(f32[3]{0:T(128)S(1)} %pad_maximum_fusion.56, f32[]{:T(128)} %get-tuple-element.4), channel_id=1, replica_groups=mesh['gx'=4,'gy'=8] {'gx','gy'}, use_global_device_ids=true, to_apply=%region_15.16 | all-reduce | flops 4 | bytes 32 | tf_op jit(solution)/shard_map/psum | solution.py:94
  335.9 5.4 %multiply_add_fusion = f32[32,32,512]{2,0,1:T(8,128)S(1)} fusion(f32[32,32,512]{2,0,1:T(8,128)} %copy-done.7, f32[32,32,512]{2,0,1:T(8,128)} %copy-done, f32[]{:T(128)S(6)} %div.56, f32[]{:T(128)S(6)} %div.57, f32[]{:T(128)S(6)} %div.58, f32[32,32,512]{2,1,0:T(8,128)} %param.4, f32[32,32,512]{2,0,1:T(8,128)} %get-tuple-element.22, f32[]{:T(128)S(6)} %sqrt.21), kind=kLoop, calls=%fused_computation.144 | loop fusion | flops 3670016 | bytes 10485776 | tf_op jit(solution)/shard_map/add | solution.py:105
  341.3 2.5 copy.29
  (100 shorter events, 29.2 us)
Async XLA Ops:
  1.6 15.5 %collective-permute-start = (f32[1,32,512]{2,0,1:T(1,128)S(1)}, f32[1,32,512]{2,0,1:T(1,128)S(1)}, u32[]{:S(2)}, u32[]{:S(2)}) collective-permute-start(f32[1,32,512]{2,0,1:T(1,128)S(1)} %copy.5), channel_id=1, source_target_pairs={{0,8},{8,16},{16,24},{1,9},{9,17},{17,25},{2,10},{10,18},{18,26},{... | collective-permute-start | bytes 196616 | tf_op jit(solution)/shard_map/ppermute | solution.py:17
  4.1 13.0 %collective-permute-start.2 = (f32[1,32,512]{2,0,1:T(1,128)S(1)}, f32[1,32,512]{2,0,1:T(1,128)S(1)}, u32[]{:S(2)}, u32[]{:S(2)}) collective-permute-start(f32[1,32,512]{2,0,1:T(1,128)S(1)} %copy.11), channel_id=1, source_target_pairs={{8,0},{16,8},{24,16},{9,1},{17,9},{25,17},{10,2},{18,10},{26,18},{... | collective-permute-start | bytes 196616 | tf_op jit(solution)/shard_map/ppermute | solution.py:19
  6.3 15.5 %collective-permute-start.1 = (f32[1,32,512]{2,0,1:T(1,128)S(1)}, f32[1,32,512]{2,0,1:T(1,128)S(1)}, u32[]{:S(2)}, u32[]{:S(2)}) collective-permute-start(f32[1,32,512]{2,0,1:T(1,128)S(1)} %copy.8), channel_id=1, source_target_pairs={{0,8},{8,16},{16,24},{1,9},{9,17},{17,25},{2,10},{10,18},{18,26},{... | collective-permute-start | bytes 196616 | tf_op jit(solution)/shard_map/ppermute | solution.py:17
  11.6 10.3 %collective-permute-start.3 = (f32[1,32,512]{2,0,1:T(1,128)S(1)}, f32[1,32,512]{2,0,1:T(1,128)S(1)}, u32[]{:S(2)}, u32[]{:S(2)}) collective-permute-start(f32[1,32,512]{2,0,1:T(1,128)S(1)} %copy.14), channel_id=1, source_target_pairs={{8,0},{16,8},{24,16},{9,1},{17,9},{25,17},{10,2},{18,10},{26,18},{... | collective-permute-start | bytes 196616 | tf_op jit(solution)/shard_map/ppermute | solution.py:19
  15.8 20.5 %copy-start.4 = (f32[32,32,512]{2,0,1:T(8,128)}, f32[32,32,512]{2,0,1:T(8,128)S(1)}, u32[]{:S(2)}) copy-start(f32[32,32,512]{2,0,1:T(8,128)S(1)} %copy.7) | copy-start | bytes 6291460
  17.1 19.2 %copy-start.9 = (f32[1,32,512]{2,0,1:T(1,128)}, f32[1,32,512]{2,0,1:T(1,128)S(1)}, u32[]{:S(2)}) copy-start(f32[1,32,512]{2,0,1:T(1,128)S(1)} %collective-permute-done.2) | copy-start | bytes 196612
  17.1 10.6 %collective-permute-start.4 = (f32[34,1,512]{2,0,1:T(8,128)S(1)}, f32[34,1,512]{2,0,1:T(8,128)S(1)}, u32[]{:S(2)}, u32[]{:S(2)}) collective-permute-start(f32[34,1,512]{2,0,1:T(8,128)S(1)} %get-tuple-element.29), channel_id=1, source_target_pairs={{0,1},{1,2},{2,3},{3,4},{4,5},{5,6},{6,7},{8,9},{9,10},{10,11},{11... | collective-permute-start | bytes 208904 | tf_op jit(solution)/shard_map/ppermute | solution.py:17
  20.6 7.2 %collective-permute-start.6 = (f32[34,1,512]{2,0,1:T(8,128)S(1)}, f32[34,1,512]{2,0,1:T(8,128)S(1)}, u32[]{:S(2)}, u32[]{:S(2)}) collective-permute-start(f32[34,1,512]{2,0,1:T(8,128)S(1)} %get-tuple-element.30), channel_id=1, source_target_pairs={{1,0},{2,1},{3,2},{4,3},{5,4},{6,5},{7,6},{9,8},{10,9},{11,10},{12... | collective-permute-start | bytes 208904 | tf_op jit(solution)/shard_map/ppermute | solution.py:19
  21.9 9.0 %collective-permute-start.5 = (f32[34,1,512]{2,0,1:T(8,128)S(1)}, f32[34,1,512]{2,0,1:T(8,128)S(1)}, u32[]{:S(2)}, u32[]{:S(2)}) collective-permute-start(f32[34,1,512]{2,0,1:T(8,128)S(1)} %get-tuple-element.31), channel_id=1, source_target_pairs={{0,1},{1,2},{2,3},{3,4},{4,5},{5,6},{6,7},{8,9},{9,10},{10,11},{11... | collective-permute-start | bytes 208904 | tf_op jit(solution)/shard_map/ppermute | solution.py:17
  26.5 6.8 %collective-permute-start.7 = (f32[34,1,512]{2,0,1:T(8,128)S(1)}, f32[34,1,512]{2,0,1:T(8,128)S(1)}, u32[]{:S(2)}, u32[]{:S(2)}) collective-permute-start(f32[34,1,512]{2,0,1:T(8,128)S(1)} %get-tuple-element.32), channel_id=1, source_target_pairs={{1,0},{2,1},{3,2},{4,3},{5,4},{6,5},{7,6},{9,8},{10,9},{11,10},{12... | collective-permute-start | bytes 208904 | tf_op jit(solution)/shard_map/ppermute | solution.py:19
  93.4 2.6 collective-permute-start.8
  94.7 5.8 %collective-permute-start.9 = (f32[1,32,512]{2,0,1:T(1,128)S(1)}, f32[1,32,512]{2,0,1:T(1,128)S(1)}, u32[]{:S(2)}, u32[]{:S(2)}) collective-permute-start(f32[1,32,512]{2,0,1:T(1,128)S(1)} %get-tuple-element.38), channel_id=1, source_target_pairs={{8,0},{16,8},{24,16},{9,1},{17,9},{25,17},{10,2},{18,10},{26,18},{... | collective-permute-start | bytes 196616 | tf_op jit(solution)/shard_map/ppermute | solution.py:19
  100.6 4.1 %collective-permute-start.10 = (f32[34,1,512]{2,0,1:T(8,128)S(1)}, f32[34,1,512]{2,0,1:T(8,128)S(1)}, u32[]{:S(2)}, u32[]{:S(2)}) collective-permute-start(f32[34,1,512]{2,0,1:T(8,128)S(1)} %get-tuple-element.27), channel_id=1, source_target_pairs={{0,1},{1,2},{2,3},{3,4},{4,5},{5,6},{6,7},{8,9},{9,10},{10,11},{11... | collective-permute-start | bytes 208904 | tf_op jit(solution)/shard_map/ppermute | solution.py:17
  102.6 9.6 %copy-start.5 = (f32[32,32,512]{2,0,1:T(8,128)S(1)}, f32[32,32,512]{2,0,1:T(8,128)}, u32[]{:S(2)}) copy-start(f32[32,32,512]{2,0,1:T(8,128)} %copy-done.4) | copy-start | bytes 6291460
  102.6 9.6 %copy-start.10 = (f32[1,32,512]{2,0,1:T(1,128)S(1)}, f32[1,32,512]{2,0,1:T(1,128)}, u32[]{:S(2)}) copy-start(f32[1,32,512]{2,0,1:T(1,128)} %copy-done.9) | copy-start | bytes 196612
  102.6 9.6 %copy-start.15 = (f32[34,1,512]{2,0,1:T(8,128)S(1)}, f32[34,1,512]{2,0,1:T(8,128)}, u32[]{:S(2)}) copy-start(f32[34,1,512]{2,0,1:T(8,128)} %copy-done.14) | copy-start | bytes 208900
  102.7 9.6 %copy-start.19 = (f32[34,1,512]{2,0,1:T(8,128)S(1)}, f32[34,1,512]{2,0,1:T(8,128)}, u32[]{:S(2)}) copy-start(f32[34,1,512]{2,0,1:T(8,128)} %copy-done.18) | copy-start | bytes 208900
  102.7 6.5 %collective-permute-start.11 = (f32[34,1,512]{2,0,1:T(8,128)S(1)}, f32[34,1,512]{2,0,1:T(8,128)S(1)}, u32[]{:S(2)}, u32[]{:S(2)}) collective-permute-start(f32[34,1,512]{2,0,1:T(8,128)S(1)} %get-tuple-element.28), channel_id=1, source_target_pairs={{1,0},{2,1},{3,2},{4,3},{5,4},{6,5},{7,6},{9,8},{10,9},{11,10},{12... | collective-permute-start | bytes 208904 | tf_op jit(solution)/shard_map/ppermute | solution.py:19
  168.8 19.0 %copy-start = (f32[32,32,512]{2,0,1:T(8,128)}, f32[32,32,512]{2,0,1:T(8,128)S(1)}, u32[]{:S(2)}) copy-start(f32[32,32,512]{2,0,1:T(8,128)S(1)} %subtract_divide_fusion.1) | copy-start | bytes 6291460
  168.9 2.6 collective-permute-start.12
  170.2 5.9 %collective-permute-start.13 = (f32[1,32,512]{2,0,1:T(1,128)S(1)}, f32[1,32,512]{2,0,1:T(1,128)S(1)}, u32[]{:S(2)}, u32[]{:S(2)}) collective-permute-start(f32[1,32,512]{2,0,1:T(1,128)S(1)} %get-tuple-element.36), channel_id=1, source_target_pairs={{8,0},{16,8},{24,16},{9,1},{17,9},{25,17},{10,2},{18,10},{26,18},{... | collective-permute-start | bytes 196616 | tf_op jit(solution)/shard_map/ppermute | solution.py:19
  176.2 4.0 %collective-permute-start.14 = (f32[34,1,512]{2,0,1:T(8,128)S(1)}, f32[34,1,512]{2,0,1:T(8,128)S(1)}, u32[]{:S(2)}, u32[]{:S(2)}) collective-permute-start(f32[34,1,512]{2,0,1:T(8,128)S(1)} %get-tuple-element.25), channel_id=1, source_target_pairs={{0,1},{1,2},{2,3},{3,4},{4,5},{5,6},{6,7},{8,9},{9,10},{10,11},{11... | collective-permute-start | bytes 208904 | tf_op jit(solution)/shard_map/ppermute | solution.py:17
  178.2 9.7 %copy-start.2 = (f32[32,32,512]{2,0,1:T(8,128)S(1)}, f32[32,32,512]{2,0,1:T(8,128)}, u32[]{:S(2)}) copy-start(f32[32,32,512]{2,0,1:T(8,128)} %get-tuple-element.22) | copy-start | bytes 6291460
  178.2 9.7 %copy-start.6 = (f32[32,32,512]{2,0,1:T(8,128)S(1)}, f32[32,32,512]{2,0,1:T(8,128)}, u32[]{:S(2)}) copy-start(f32[32,32,512]{2,0,1:T(8,128)} %copy-done.4) | copy-start | bytes 6291460
  178.2 9.7 %copy-start.11 = (f32[1,32,512]{2,0,1:T(1,128)S(1)}, f32[1,32,512]{2,0,1:T(1,128)}, u32[]{:S(2)}) copy-start(f32[1,32,512]{2,0,1:T(1,128)} %copy-done.9) | copy-start | bytes 196612
  178.2 9.7 %copy-start.16 = (f32[34,1,512]{2,0,1:T(8,128)S(1)}, f32[34,1,512]{2,0,1:T(8,128)}, u32[]{:S(2)}) copy-start(f32[34,1,512]{2,0,1:T(8,128)} %copy-done.14) | copy-start | bytes 208900
  178.2 9.7 %copy-start.20 = (f32[34,1,512]{2,0,1:T(8,128)S(1)}, f32[34,1,512]{2,0,1:T(8,128)}, u32[]{:S(2)}) copy-start(f32[34,1,512]{2,0,1:T(8,128)} %copy-done.18) | copy-start | bytes 208900
  178.2 6.6 %collective-permute-start.15 = (f32[34,1,512]{2,0,1:T(8,128)S(1)}, f32[34,1,512]{2,0,1:T(8,128)S(1)}, u32[]{:S(2)}, u32[]{:S(2)}) collective-permute-start(f32[34,1,512]{2,0,1:T(8,128)S(1)} %get-tuple-element.26), channel_id=1, source_target_pairs={{1,0},{2,1},{3,2},{4,3},{5,4},{6,5},{7,6},{9,8},{10,9},{11,10},{12... | collective-permute-start | bytes 208904 | tf_op jit(solution)/shard_map/ppermute | solution.py:19
  248.7 2.6 collective-permute-start.16
  250.0 5.9 %collective-permute-start.17 = (f32[1,32,512]{2,0,1:T(1,128)S(1)}, f32[1,32,512]{2,0,1:T(1,128)S(1)}, u32[]{:S(2)}, u32[]{:S(2)}) collective-permute-start(f32[1,32,512]{2,0,1:T(1,128)S(1)} %get-tuple-element.34), channel_id=1, source_target_pairs={{8,0},{16,8},{24,16},{9,1},{17,9},{25,17},{10,2},{18,10},{26,18},{... | collective-permute-start | bytes 196616 | tf_op jit(solution)/shard_map/ppermute | solution.py:19
  256.6 9.0 %collective-permute-start.18 = (f32[34,1,512]{2,0,1:T(8,128)}, f32[34,1,512]{2,0,1:T(8,128)}, u32[]{:S(2)}, u32[]{:S(2)}) collective-permute-start(f32[34,1,512]{2,0,1:T(8,128)} %get-tuple-element.23), channel_id=1, source_target_pairs={{0,1},{1,2},{2,3},{3,4},{4,5},{5,6},{6,7},{8,9},{9,10},{10,11},{11... | collective-permute-start | bytes 208904 | tf_op jit(solution)/shard_map/ppermute | solution.py:17
  259.2 6.6 %collective-permute-start.19 = (f32[34,1,512]{2,0,1:T(8,128)}, f32[34,1,512]{2,0,1:T(8,128)}, u32[]{:S(2)}, u32[]{:S(2)}) collective-permute-start(f32[34,1,512]{2,0,1:T(8,128)} %get-tuple-element.24), channel_id=1, source_target_pairs={{1,0},{2,1},{3,2},{4,3},{5,4},{6,5},{7,6},{9,8},{10,9},{11,10},{12... | collective-permute-start | bytes 208904 | tf_op jit(solution)/shard_map/ppermute | solution.py:19
  (14 other events, 74.9 us)
where the time goes:
time: 347 us; the launch traced here: 345 us
  blocking collectives  173 us (50%)
  other arithmetic  79 us (23%)
  starting transfers between devices  39.9 us (11%)
  waiting for transfers between devices  26.3 us (8%)
  between operations  16.7 us (5%)
  local copies, waits for them, and re-layouts  10.4 us (3%)
    psum x3, blocking collectives, local(): lax.psum((local_dots, jnp.sum(vector * vector)), ('gx', 'gy'))  128 us
    psum x1, blocking collectives, global_norm(): return jnp.sqrt(lax.psum(jnp.sum(vector * vector), ('gx', 'gy')))  44.5 us
    ppermute x10, starting transfers between devices, with_halo(): lax.ppermute(tail, axis, [(i, (i + 1) % count) for i in range(ends)])  26 us
    ppermute x10, waiting for transfers between devices, with_halo(): lax.ppermute(head, axis, [((i + 1) % count, i) for i in range(ends)])  25.5 us
    reduce_sum x2, other arithmetic, local(): jnp.sum(vector * basis[earlier])  16.9 us
    concatenate x5, other arithmetic, with_halo(): jnp.concatenate([lax.ppermute(tail, axis, [(i, (i + 1) % count) for i in...  16.7 us
    reduce_sum x1, other arithmetic, local(): jnp.sum(vector * vector)  14.5 us
    ppermute x10, starting transfers between devices, with_halo(): lax.ppermute(head, axis, [((i + 1) % count, i) for i in range(ends)])  13.8 us
  transfers between devices with their start and end apart: 20, of which 9 were waited for; matrix products, arithmetic and copies ran while one was open for 2% of the time, Pallas kernels for 0%

commit v1 on v0

--- a/solution.py
+++ b/solution.py
@@ -2,6 +2,7 @@
 import jax.numpy as jnp
 from jax import lax
 from jax.sharding import PartitionSpec as P
+from jax.lax import psum
 
 M = 3
 
@@ -91,7 +92,7 @@
     for column in range(M):
         vector = stencil(basis[column], kappa_pad)
         local_dots = jnp.stack([jnp.sum(vector * basis[earlier]) for earlier in range(column + 1)])
-        coeff_all, squares = lax.psum((local_dots, jnp.sum(vector * vector)), ("gx", "gy"))
+        coeff_all, squares = psum(psum((local_dots, jnp.sum(vector * vector)), "gy"), "gx")
         for earlier in range(column + 1):
             vector = vector - coeff_all[earlier] * basis[earlier]
         entries = [coeff_all[earlier] for earlier in range(column + 1)]

time: 347 us -> 297 us (0.86)
  blocking collectives: 173 us -> 125 us
    psum x3 -> x6, blocking collectives: 128 us -> 81 us  [the longest x3 60.1 us: local(): psum((local_dots, jnp.sum(vector * vector)), 'gy')]
  transfers between devices with their start and end apart: 20 -> 20, of which waited for: 9 -> 9; matrix products, arithmetic and copies ran while one was open for 2% -> 3% of each run, Pallas kernels for 0% -> 0%
where the time goes in v1:
time: 297 us; the launch traced here: 296 us
  blocking collectives  125 us (42%)
  other arithmetic  78.6 us (26%)
  starting transfers between devices  41.3 us (14%)
  waiting for transfers between devices  23.8 us (8%)
  between operations  16.5 us (6%)
  local copies, waits for them, and re-layouts  10.3 us (3%)
    psum x3, blocking collectives, local(): psum((local_dots, jnp.sum(vector * vector)), 'gy')  60.1 us
    psum x1, blocking collectives, global_norm(): return jnp.sqrt(lax.psum(jnp.sum(vector * vector), ('gx', 'gy')))  44.4 us
    ppermute x10, starting transfers between devices, with_halo(): lax.ppermute(tail, axis, [(i, (i + 1) % count) for i in range(ends)])  27.4 us
    ppermute x10, waiting for transfers between devices, with_halo(): lax.ppermute(head, axis, [((i + 1) % count, i) for i in range(ends)])  23 us
    psum x3, blocking collectives, local(): psum(psum((local_dots, jnp.sum(vector * vector)), 'gy'), 'gx')  20.9 us
    reduce_sum x2, other arithmetic, local(): jnp.sum(vector * basis[earlier])  17 us
    concatenate x5, other arithmetic, with_halo(): jnp.concatenate([lax.ppermute(tail, axis, [(i, (i + 1) % count) for i in...  16.7 us
    reduce_sum x1, other arithmetic, local(): jnp.sum(vector * vector)  13.9 us
  transfers between devices with their start and end apart: 20, of which 9 were waited for; matrix products, arithmetic and copies ran while one was open for 3% of the time, Pallas kernels for 0%

profile of v1, /device:TPU:0, one launch (start us, length us, event | category | flops | bytes accessed | tf_op | source)
XLA Modules:
  0.0 295.9 jit_solution(9604738409408922633)
XLA Ops:
  1.6 2.4 collective-permute-start
  6.3 5.2 %collective-permute-start.1 = (f32[1,32,512]{2,0,1:T(1,128)S(1)}, f32[1,32,512]{2,0,1:T(1,128)S(1)}, u32[]{:S(2)}, u32[]{:S(2)}) collective-permute-start(f32[1,32,512]{2,0,1:T(1,128)S(1)} %copy.8), channel_id=1, source_target_pairs={{0,8},{8,16},{16,24},{1,9},{9,17},{17,25},{2,10},{10,18},{18,26},{... | collective-permute-start | bytes 196616 | tf_op jit(solution)/shard_map/ppermute | solution.py:18
  13.0 2.8 copy.7
  17.1 3.4 %collective-permute-start.4 = (f32[34,1,512]{2,0,1:T(8,128)S(1)}, f32[34,1,512]{2,0,1:T(8,128)S(1)}, u32[]{:S(2)}, u32[]{:S(2)}) collective-permute-start(f32[34,1,512]{2,0,1:T(8,128)S(1)} %get-tuple-element.35), channel_id=1, source_target_pairs={{0,1},{1,2},{2,3},{3,4},{4,5},{5,6},{6,7},{8,9},{9,10},{10,11},{11... | collective-permute-start | bytes 208904 | tf_op jit(solution)/shard_map/ppermute | solution.py:18
  21.9 4.6 %collective-permute-start.5 = (f32[34,1,512]{2,0,1:T(8,128)S(1)}, f32[34,1,512]{2,0,1:T(8,128)S(1)}, u32[]{:S(2)}, u32[]{:S(2)}) collective-permute-start(f32[34,1,512]{2,0,1:T(8,128)S(1)} %get-tuple-element.37), channel_id=1, source_target_pairs={{0,1},{1,2},{2,3},{3,4},{4,5},{5,6},{6,7},{8,9},{9,10},{10,11},{11... | collective-permute-start | bytes 208904 | tf_op jit(solution)/shard_map/ppermute | solution.py:18
  27.8 3.0 %select_maximum_fusion.16 = f32[34,34,514]{2,0,1:T(8,128)S(1)} fusion(f32[34,1,512]{2,0,1:T(8,128)S(1)} %collective-permute-done.6, f32[34,1,512]{2,0,1:T(8,128)S(1)} %collective-permute-done.4, f32[1,32,512]{2,0,1:T(1,128)S(1)} %collective-permute-done.2, f32[32,32,512]{2,0,1:T(8,128)S(1)} %copy.7, f32[1,32,512]{2,0,1:T(1,128)S(1)} %collective-permute-done), kind=kLoop, calls=%fused_computation.18 | loop fusion | flops 7130208 | bytes 4744224 | tf_op jit(solution)/shard_map/concatenate | solution.py:16
  30.9 2.4 collective-permute-done.7
  33.3 3.0 %select_maximum_fusion.12 = f32[34,34,514]{2,0,1:T(8,128)S(1)} fusion(f32[34,1,512]{2,0,1:T(8,128)S(1)} %collective-permute-done.7, f32[34,1,512]{2,0,1:T(8,128)S(1)} %collective-permute-done.5, f32[1,32,512]{2,0,1:T(1,128)S(1)} %collective-permute-done.3, f32[32,32,512]{2,0,1:T(8,128)S(1)} %copy.28, f32[1,32,512]{2,0,1:T(1,128)S(1)} %collective-permute-done.1), kind=kLoop, calls=%fused_computation.14 | loop fusion | flops 7130208 | bytes 4744224 | tf_op jit(solution)/shard_map/concatenate | solution.py:16
  36.4 10.0 %multiply_reduce_fusion.9 = (f32[]{:T(128)}, f32[32,32,512]{2,0,1:T(8,128)}) fusion(f32[32,32,512]{2,0,1:T(8,128)S(1)} %copy.28, f32[34,34,514]{2,0,1:T(8,128)S(1)} %select_maximum_fusion.12, f32[32,32,512]{2,0,1:T(8,128)S(1)} %copy.7, f32[34,34,514]{2,0,1:T(8,128)S(1)} %select_maximum_fusion.16, f32[34,1,512]{2,0,1:T(8,128)S(1)} %collective-permute-done.7, ...), kind=kLoop, calls=%fused_computation.156 | loop fusion | flops 25165824 | bytes 17317892 | tf_op jit(solution)/shard_map/reduce_sum | solution.py:52
  46.3 44.4 %psum.91 = f32[]{:T(128)} all-reduce(f32[]{:T(128)} %get-tuple-element.27), channel_id=1, replica_groups=mesh['gx'=4,'gy'=8] {'gx','gy'}, use_global_device_ids=true, to_apply=%region_1.2 | all-reduce | flops 1 | bytes 8 | tf_op jit(solution)/shard_map/psum | solution.py:52
  96.0 4.5 %collective-permute-done.9 = f32[1,32,512]{2,0,1:T(1,128)S(1)} collective-permute-done((f32[1,32,512]{2,0,1:T(1,128)S(1)}, f32[1,32,512]{2,0,1:T(1,128)S(1)}, u32[]{:S(2)}, u32[]{:S(2)}) %collective-permute-start.9) | collective-permute-done | bytes 65568 | tf_op jit(solution)/shard_map/ppermute | solution.py:20
  104.7 4.5 %collective-permute-done.11 = f32[34,1,512]{2,0,1:T(8,128)S(1)} collective-permute-done((f32[34,1,512]{2,0,1:T(8,128)S(1)}, f32[34,1,512]{2,0,1:T(8,128)S(1)}, u32[]{:S(2)}, u32[]{:S(2)}) %collective-permute-start.11) | collective-permute-done | bytes 69664 | tf_op jit(solution)/shard_map/ppermute | solution.py:20
  109.1 3.0 %select_maximum_fusion.8 = f32[34,34,514]{2,0,1:T(8,128)S(1)} fusion(f32[34,1,512]{2,0,1:T(8,128)S(1)} %collective-permute-done.11, f32[34,1,512]{2,0,1:T(8,128)S(1)} %collective-permute-done.10, f32[1,32,512]{2,0,1:T(1,128)S(1)} %collective-permute-done.9, f32[32,32,512]{2,0,1:T(8,128)S(1)} %broadcast_divide_fusion, f32[1,32,512]{2,0,1:T(1,128)S(1)} %collective-permute-done.8), kind=kLoop, calls=%fused_computation.10 | loop fusion | flops 7130208 | bytes 4744224 | tf_op jit(solution)/shard_map/concatenate | solution.py:16
  112.2 8.4 %multiply_reduce_fusion.8 = (f32[]{:T(128)}, f32[]{:T(128)}, f32[32,32,512]{2,0,1:T(8,128)}) fusion(f32[32,32,512]{2,0,1:T(8,128)S(1)} %broadcast_divide_fusion, f32[34,34,514]{2,0,1:T(8,128)S(1)} %select_maximum_fusion.8, f32[32,32,512]{2,0,1:T(8,128)S(1)} %copy-done.5, f32[34,34,514]{2,0,1:T(8,128)S(1)} %select_maximum_fusion.16, ...), kind=kLoop, calls=%fused_computation.155 | loop fusion | flops 25690112 | bytes 15220744 | tf_op jit(solution)/shard_map/reduce_sum | solution.py:94
  120.6 20.5 %all-reduce.7 = (f32[]{:T(128)}, f32[1]{0:T(128)}) all-reduce(f32[]{:T(128)} %get-tuple-element.12, f32[1]{0:T(128)} %bitcast), channel_id=1, replica_groups=mesh['gx'=4,'gy'=8] {'gy'}, use_global_device_ids=true, to_apply=%region_6.7 | all-reduce | flops 2 | bytes 16 | tf_op jit(solution)/shard_map/psum | solution.py:95
  141.1 6.9 %all-reduce.10 = (f32[]{:T(128)}, f32[1]{0:T(128)}) all-reduce(f32[]{:T(128)} %get-tuple-element.17, f32[1]{0:T(128)} %get-tuple-element.18), channel_id=1, replica_groups=mesh['gx'=4,'gy'=8] {'gx'}, use_global_device_ids=true, to_apply=%region_7.8 | all-reduce | flops 2 | bytes 16 | tf_op jit(solution)/shard_map/psum | solution.py:95
  149.9 3.4 %subtract_divide_fusion.1 = f32[32,32,512]{2,0,1:T(8,128)S(1)} fusion(f32[32,32,512]{2,0,1:T(8,128)} %get-tuple-element.26, f32[]{:T(128)S(6)} %sqrt.22, f32[]{:T(128)} %bitcast.1, f32[32,32,512]{2,0,1:T(8,128)} %get-tuple-element.28, f32[]{:T(128)S(6)} %sqrt.21), kind=kLoop, calls=%fused_computation.153 | loop fusion | flops 2097152 | bytes 6291468 | tf_op jit(solution)/shard_map/div | solution.py:102
  157.0 3.3 %collective-permute-done.13 = f32[1,32,512]{2,0,1:T(1,128)S(1)} collective-permute-done((f32[1,32,512]{2,0,1:T(1,128)S(1)}, f32[1,32,512]{2,0,1:T(1,128)S(1)}, u32[]{:S(2)}, u32[]{:S(2)}) %collective-permute-start.13) | collective-permute-done | bytes 65568 | tf_op jit(solution)/shard_map/ppermute | solution.py:20
  163.7 4.6 %collective-permute-done.15 = f32[34,1,512]{2,0,1:T(8,128)S(1)} collective-permute-done((f32[34,1,512]{2,0,1:T(8,128)S(1)}, f32[34,1,512]{2,0,1:T(8,128)S(1)}, u32[]{:S(2)}, u32[]{:S(2)}) %collective-permute-start.15) | collective-permute-done | bytes 69664 | tf_op jit(solution)/shard_map/ppermute | solution.py:20
  168.3 3.0 %select_maximum_fusion.4 = f32[34,34,514]{2,0,1:T(8,128)S(1)} fusion(f32[34,1,512]{2,0,1:T(8,128)S(1)} %collective-permute-done.15, f32[34,1,512]{2,0,1:T(8,128)S(1)} %collective-permute-done.14, f32[1,32,512]{2,0,1:T(1,128)S(1)} %collective-permute-done.13, f32[32,32,512]{2,0,1:T(8,128)S(1)} %subtract_divide_fusion.1, ...), kind=kLoop, calls=%fused_computation.6 | loop fusion | flops 7130208 | bytes 4744224 | tf_op jit(solution)/shard_map/concatenate | solution.py:16
  171.4 8.6 %multiply_reduce_fusion.6 = (f32[]{:T(128)}, f32[]{:T(128)}, f32[]{:T(128)}, f32[32,32,512]{2,0,1:T(8,128)}) fusion(f32[32,32,512]{2,0,1:T(8,128)S(1)} %subtract_divide_fusion.1, f32[34,34,514]{2,0,1:T(8,128)S(1)} %select_maximum_fusion.4, f32[32,32,512]{2,0,1:T(8,128)S(1)} %copy-done.6, f32[34,34,514]{2,0,1:T(8,128)S(1)} %select_maximum_fusion.16, ...), kind=kLoop, calls=%fused_computation.152 | loop fusion | flops 27262976 | bytes 17317904 | tf_op jit(solution)/shard_map/reduce_sum | solution.py:94
  181.5 19.6 %all-reduce.6 = (f32[]{:T(128)}, f32[2]{0:T(128)S(1)}) all-reduce(f32[]{:T(128)} %get-tuple-element.9, f32[2]{0:T(128)S(1)} %pad_maximum_fusion.55), channel_id=1, replica_groups=mesh['gx'=4,'gy'=8] {'gy'}, use_global_device_ids=true, to_apply=%region_13.14 | all-reduce | flops 3 | bytes 24 | tf_op jit(solution)/shard_map/psum | solution.py:95
  201.0 7.0 %all-reduce.9 = (f32[]{:T(128)}, f32[2]{0:T(128)S(1)}) all-reduce(f32[]{:T(128)} %get-tuple-element.15, f32[2]{0:T(128)S(1)} %get-tuple-element.16), channel_id=1, replica_groups=mesh['gx'=4,'gy'=8] {'gx'}, use_global_device_ids=true, to_apply=%region_14.15 | all-reduce | flops 3 | bytes 24 | tf_op jit(solution)/shard_map/psum | solution.py:95
  210.7 5.0 %subtract_divide_fusion = f32[32,32,512]{2,0,1:T(8,128)S(1)} fusion(f32[32,32,512]{2,0,1:T(8,128)} %copy-done, f32[32,32,512]{2,0,1:T(8,128)} %get-tuple-element.25, f32[]{:T(128)S(6)} %sqrt.24, f32[]{:T(128)} %bitcast.6, f32[]{:T(128)} %bitcast.5, f32[32,32,512]{2,0,1:T(8,128)} %get-tuple-element.28, f32[]{:T(128)S(6)} %sqrt.21), kind=kLoop, calls=%fused_computation.149 | loop fusion | flops 3145728 | bytes 8388624 | tf_op jit(solution)/shard_map/div | solution.py:102
  219.4 3.3 %collective-permute-done.17 = f32[1,32,512]{2,0,1:T(1,128)S(1)} collective-permute-done((f32[1,32,512]{2,0,1:T(1,128)S(1)}, f32[1,32,512]{2,0,1:T(1,128)S(1)}, u32[]{:S(2)}, u32[]{:S(2)}) %collective-permute-start.17) | collective-permute-done | bytes 65568 | tf_op jit(solution)/shard_map/ppermute | solution.py:20
  223.4 2.8 collective-permute-start.18
  232.8 4.6 %select_maximum_fusion = f32[34,34,514]{2,0,1:T(8,128)S(1)} fusion(f32[34,1,512]{2,0,1:T(8,128)} %collective-permute-done.19, f32[34,1,512]{2,0,1:T(8,128)} %collective-permute-done.18, f32[1,32,512]{2,0,1:T(1,128)} %copy-done.24, f32[32,32,512]{2,0,1:T(8,128)} %copy-done.7, f32[1,32,512]{2,0,1:T(1,128)} %copy-done.22), kind=kLoop, calls=%fused_computation.2 | loop fusion | flops 7130208 | bytes 4744224 | tf_op jit(solution)/shard_map/concatenate | solution.py:16
  237.5 13.9 %multiply_reduce_fusion = (f32[]{:T(128)}, f32[]{:T(128)}, f32[]{:T(128)}, f32[]{:T(128)}) fusion(f32[32,32,512]{2,0,1:T(8,128)} %copy-done.7, f32[32,32,512]{2,0,1:T(8,128)S(1)} %copy-done.1, f32[34,34,514]{2,0,1:T(8,128)S(1)} %select_maximum_fusion, f32[32,32,512]{2,0,1:T(8,128)} %copy-done.4, f32[34,34,514]{2,0,1:T(8,128)S(1)} %select_maximum_fusion.16, ...), kind=kLoop, calls=%fused_computation.145 | loop fusion | flops 28311552 | bytes 17317908 | tf_op jit(solution)/shard_map/reduce_sum | solution.py:95
  253.4 20.1 %all-reduce.5 = (f32[3]{0:T(128)S(1)}, f32[]{:T(128)}) all-reduce(f32[3]{0:T(128)S(1)} %pad_maximum_fusion.56, f32[]{:T(128)} %get-tuple-element.4), channel_id=1, replica_groups=mesh['gx'=4,'gy'=8] {'gy'}, use_global_device_ids=true, to_apply=%region_19.20 | all-reduce | flops 4 | bytes 32 | tf_op jit(solution)/shard_map/psum | solution.py:95
  273.5 6.9 %all-reduce.8 = (f32[3]{0:T(128)S(1)}, f32[]{:T(128)}) all-reduce(f32[3]{0:T(128)S(1)} %get-tuple-element.13, f32[]{:T(128)} %get-tuple-element.14), channel_id=1, replica_groups=mesh['gx'=4,'gy'=8] {'gx'}, use_global_device_ids=true, to_apply=%region_20.21 | all-reduce | flops 4 | bytes 32 | tf_op jit(solution)/shard_map/psum | solution.py:95
  286.9 5.4 %multiply_add_fusion = f32[32,32,512]{2,0,1:T(8,128)S(1)} fusion(f32[32,32,512]{2,0,1:T(8,128)} %copy-done.7, f32[32,32,512]{2,0,1:T(8,128)} %copy-done, f32[]{:T(128)S(6)} %div.56, f32[]{:T(128)S(6)} %div.57, f32[]{:T(128)S(6)} %div.58, f32[32,32,512]{2,1,0:T(8,128)} %param.4, f32[32,32,512]{2,0,1:T(8,128)} %get-tuple-element.28, f32[]{:T(128)S(6)} %sqrt.21), kind=kLoop, calls=%fused_computation.144 | loop fusion | flops 3670016 | bytes 10485776 | tf_op jit(solution)/shard_map/add | solution.py:106
  292.3 2.5 copy.29
  (103 shorter events, 36.5 us)
Async XLA Ops:
  1.6 15.5 %collective-permute-start = (f32[1,32,512]{2,0,1:T(1,128)S(1)}, f32[1,32,512]{2,0,1:T(1,128)S(1)}, u32[]{:S(2)}, u32[]{:S(2)}) collective-permute-start(f32[1,32,512]{2,0,1:T(1,128)S(1)} %copy.5), channel_id=1, source_target_pairs={{0,8},{8,16},{16,24},{1,9},{9,17},{17,25},{2,10},{10,18},{18,26},{... | collective-permute-start | bytes 196616 | tf_op jit(solution)/shard_map/ppermute | solution.py:18
  4.1 13.0 %collective-permute-start.2 = (f32[1,32,512]{2,0,1:T(1,128)S(1)}, f32[1,32,512]{2,0,1:T(1,128)S(1)}, u32[]{:S(2)}, u32[]{:S(2)}) collective-permute-start(f32[1,32,512]{2,0,1:T(1,128)S(1)} %copy.11), channel_id=1, source_target_pairs={{8,0},{16,8},{24,16},{9,1},{17,9},{25,17},{10,2},{18,10},{26,18},{... | collective-permute-start | bytes 196616 | tf_op jit(solution)/shard_map/ppermute | solution.py:20
  6.3 15.5 %collective-permute-start.1 = (f32[1,32,512]{2,0,1:T(1,128)S(1)}, f32[1,32,512]{2,0,1:T(1,128)S(1)}, u32[]{:S(2)}, u32[]{:S(2)}) collective-permute-start(f32[1,32,512]{2,0,1:T(1,128)S(1)} %copy.8), channel_id=1, source_target_pairs={{0,8},{8,16},{16,24},{1,9},{9,17},{17,25},{2,10},{10,18},{18,26},{... | collective-permute-start | bytes 196616 | tf_op jit(solution)/shard_map/ppermute | solution.py:18
  11.6 10.3 %collective-permute-start.3 = (f32[1,32,512]{2,0,1:T(1,128)S(1)}, f32[1,32,512]{2,0,1:T(1,128)S(1)}, u32[]{:S(2)}, u32[]{:S(2)}) collective-permute-start(f32[1,32,512]{2,0,1:T(1,128)S(1)} %copy.14), channel_id=1, source_target_pairs={{8,0},{16,8},{24,16},{9,1},{17,9},{25,17},{10,2},{18,10},{26,18},{... | collective-permute-start | bytes 196616 | tf_op jit(solution)/shard_map/ppermute | solution.py:20
  15.8 20.5 %copy-start.4 = (f32[32,32,512]{2,0,1:T(8,128)}, f32[32,32,512]{2,0,1:T(8,128)S(1)}, u32[]{:S(2)}) copy-start(f32[32,32,512]{2,0,1:T(8,128)S(1)} %copy.7) | copy-start | bytes 6291460
  17.1 19.2 %copy-start.9 = (f32[1,32,512]{2,0,1:T(1,128)}, f32[1,32,512]{2,0,1:T(1,128)S(1)}, u32[]{:S(2)}) copy-start(f32[1,32,512]{2,0,1:T(1,128)S(1)} %collective-permute-done.2) | copy-start | bytes 196612
  17.1 10.6 %collective-permute-start.4 = (f32[34,1,512]{2,0,1:T(8,128)S(1)}, f32[34,1,512]{2,0,1:T(8,128)S(1)}, u32[]{:S(2)}, u32[]{:S(2)}) collective-permute-start(f32[34,1,512]{2,0,1:T(8,128)S(1)} %get-tuple-element.35), channel_id=1, source_target_pairs={{0,1},{1,2},{2,3},{3,4},{4,5},{5,6},{6,7},{8,9},{9,10},{10,11},{11... | collective-permute-start | bytes 208904 | tf_op jit(solution)/shard_map/ppermute | solution.py:18
  20.6 7.2 %collective-permute-start.6 = (f32[34,1,512]{2,0,1:T(8,128)S(1)}, f32[34,1,512]{2,0,1:T(8,128)S(1)}, u32[]{:S(2)}, u32[]{:S(2)}) collective-permute-start(f32[34,1,512]{2,0,1:T(8,128)S(1)} %get-tuple-element.36), channel_id=1, source_target_pairs={{1,0},{2,1},{3,2},{4,3},{5,4},{6,5},{7,6},{9,8},{10,9},{11,10},{12... | collective-permute-start | bytes 208904 | tf_op jit(solution)/shard_map/ppermute | solution.py:20
  21.9 9.0 %collective-permute-start.5 = (f32[34,1,512]{2,0,1:T(8,128)S(1)}, f32[34,1,512]{2,0,1:T(8,128)S(1)}, u32[]{:S(2)}, u32[]{:S(2)}) collective-permute-start(f32[34,1,512]{2,0,1:T(8,128)S(1)} %get-tuple-element.37), channel_id=1, source_target_pairs={{0,1},{1,2},{2,3},{3,4},{4,5},{5,6},{6,7},{8,9},{9,10},{10,11},{11... | collective-permute-start | bytes 208904 | tf_op jit(solution)/shard_map/ppermute | solution.py:18
  26.5 6.8 %collective-permute-start.7 = (f32[34,1,512]{2,0,1:T(8,128)S(1)}, f32[34,1,512]{2,0,1:T(8,128)S(1)}, u32[]{:S(2)}, u32[]{:S(2)}) collective-permute-start(f32[34,1,512]{2,0,1:T(8,128)S(1)} %get-tuple-element.38), channel_id=1, source_target_pairs={{1,0},{2,1},{3,2},{4,3},{5,4},{6,5},{7,6},{9,8},{10,9},{11,10},{12... | collective-permute-start | bytes 208904 | tf_op jit(solution)/shard_map/ppermute | solution.py:20
  93.4 2.6 collective-permute-start.8
  94.7 5.8 %collective-permute-start.9 = (f32[1,32,512]{2,0,1:T(1,128)S(1)}, f32[1,32,512]{2,0,1:T(1,128)S(1)}, u32[]{:S(2)}, u32[]{:S(2)}) collective-permute-start(f32[1,32,512]{2,0,1:T(1,128)S(1)} %get-tuple-element.44), channel_id=1, source_target_pairs={{8,0},{16,8},{24,16},{9,1},{17,9},{25,17},{10,2},{18,10},{26,18},{... | collective-permute-start | bytes 196616 | tf_op jit(solution)/shard_map/ppermute | solution.py:20
  100.6 4.1 %collective-permute-start.10 = (f32[34,1,512]{2,0,1:T(8,128)S(1)}, f32[34,1,512]{2,0,1:T(8,128)S(1)}, u32[]{:S(2)}, u32[]{:S(2)}) collective-permute-start(f32[34,1,512]{2,0,1:T(8,128)S(1)} %get-tuple-element.33), channel_id=1, source_target_pairs={{0,1},{1,2},{2,3},{3,4},{4,5},{5,6},{6,7},{8,9},{9,10},{10,11},{11... | collective-permute-start | bytes 208904 | tf_op jit(solution)/shard_map/ppermute | solution.py:18
  102.6 9.5 %copy-start.5 = (f32[32,32,512]{2,0,1:T(8,128)S(1)}, f32[32,32,512]{2,0,1:T(8,128)}, u32[]{:S(2)}) copy-start(f32[32,32,512]{2,0,1:T(8,128)} %copy-done.4) | copy-start | bytes 6291460
  102.7 9.5 %copy-start.10 = (f32[1,32,512]{2,0,1:T(1,128)S(1)}, f32[1,32,512]{2,0,1:T(1,128)}, u32[]{:S(2)}) copy-start(f32[1,32,512]{2,0,1:T(1,128)} %copy-done.9) | copy-start | bytes 196612
  102.7 9.5 %copy-start.15 = (f32[34,1,512]{2,0,1:T(8,128)S(1)}, f32[34,1,512]{2,0,1:T(8,128)}, u32[]{:S(2)}) copy-start(f32[34,1,512]{2,0,1:T(8,128)} %copy-done.14) | copy-start | bytes 208900
  102.7 9.5 %copy-start.19 = (f32[34,1,512]{2,0,1:T(8,128)S(1)}, f32[34,1,512]{2,0,1:T(8,128)}, u32[]{:S(2)}) copy-start(f32[34,1,512]{2,0,1:T(8,128)} %copy-done.18) | copy-start | bytes 208900
  102.7 6.5 %collective-permute-start.11 = (f32[34,1,512]{2,0,1:T(8,128)S(1)}, f32[34,1,512]{2,0,1:T(8,128)S(1)}, u32[]{:S(2)}, u32[]{:S(2)}) collective-permute-start(f32[34,1,512]{2,0,1:T(8,128)S(1)} %get-tuple-element.34), channel_id=1, source_target_pairs={{1,0},{2,1},{3,2},{4,3},{5,4},{6,5},{7,6},{9,8},{10,9},{11,10},{12... | collective-permute-start | bytes 208904 | tf_op jit(solution)/shard_map/ppermute | solution.py:20
  153.3 18.0 %copy-start = (f32[32,32,512]{2,0,1:T(8,128)}, f32[32,32,512]{2,0,1:T(8,128)S(1)}, u32[]{:S(2)}) copy-start(f32[32,32,512]{2,0,1:T(8,128)S(1)} %subtract_divide_fusion.1) | copy-start | bytes 6291460
  153.5 3.6 %collective-permute-start.12 = (f32[1,32,512]{2,0,1:T(1,128)S(1)}, f32[1,32,512]{2,0,1:T(1,128)S(1)}, u32[]{:S(2)}, u32[]{:S(2)}) collective-permute-start(f32[1,32,512]{2,0,1:T(1,128)S(1)} %get-tuple-element.41), channel_id=1, source_target_pairs={{0,8},{8,16},{16,24},{1,9},{9,17},{17,25},{2,10},{10,18},{18,26},{... | collective-permute-start | bytes 196616 | tf_op jit(solution)/shard_map/ppermute | solution.py:18
  155.7 4.6 %collective-permute-start.13 = (f32[1,32,512]{2,0,1:T(1,128)S(1)}, f32[1,32,512]{2,0,1:T(1,128)S(1)}, u32[]{:S(2)}, u32[]{:S(2)}) collective-permute-start(f32[1,32,512]{2,0,1:T(1,128)S(1)} %get-tuple-element.42), channel_id=1, source_target_pairs={{8,0},{16,8},{24,16},{9,1},{17,9},{25,17},{10,2},{18,10},{26,18},{... | collective-permute-start | bytes 196616 | tf_op jit(solution)/shard_map/ppermute | solution.py:20
  160.4 3.3 %collective-permute-start.14 = (f32[34,1,512]{2,0,1:T(8,128)S(1)}, f32[34,1,512]{2,0,1:T(8,128)S(1)}, u32[]{:S(2)}, u32[]{:S(2)}) collective-permute-start(f32[34,1,512]{2,0,1:T(8,128)S(1)} %get-tuple-element.31), channel_id=1, source_target_pairs={{0,1},{1,2},{2,3},{3,4},{4,5},{5,6},{6,7},{8,9},{9,10},{10,11},{11... | collective-permute-start | bytes 208904 | tf_op jit(solution)/shard_map/ppermute | solution.py:18
  161.7 9.7 %copy-start.2 = (f32[32,32,512]{2,0,1:T(8,128)S(1)}, f32[32,32,512]{2,0,1:T(8,128)}, u32[]{:S(2)}) copy-start(f32[32,32,512]{2,0,1:T(8,128)} %get-tuple-element.28) | copy-start | bytes 6291460
  161.7 9.7 %copy-start.6 = (f32[32,32,512]{2,0,1:T(8,128)S(1)}, f32[32,32,512]{2,0,1:T(8,128)}, u32[]{:S(2)}) copy-start(f32[32,32,512]{2,0,1:T(8,128)} %copy-done.4) | copy-start | bytes 6291460
  161.7 9.7 %copy-start.11 = (f32[1,32,512]{2,0,1:T(1,128)S(1)}, f32[1,32,512]{2,0,1:T(1,128)}, u32[]{:S(2)}) copy-start(f32[1,32,512]{2,0,1:T(1,128)} %copy-done.9) | copy-start | bytes 196612
  161.7 9.7 %copy-start.16 = (f32[34,1,512]{2,0,1:T(8,128)S(1)}, f32[34,1,512]{2,0,1:T(8,128)}, u32[]{:S(2)}) copy-start(f32[34,1,512]{2,0,1:T(8,128)} %copy-done.14) | copy-start | bytes 208900
  161.7 9.7 %copy-start.20 = (f32[34,1,512]{2,0,1:T(8,128)S(1)}, f32[34,1,512]{2,0,1:T(8,128)}, u32[]{:S(2)}) copy-start(f32[34,1,512]{2,0,1:T(8,128)} %copy-done.18) | copy-start | bytes 208900
  161.7 6.6 %collective-permute-start.15 = (f32[34,1,512]{2,0,1:T(8,128)S(1)}, f32[34,1,512]{2,0,1:T(8,128)S(1)}, u32[]{:S(2)}, u32[]{:S(2)}) collective-permute-start(f32[34,1,512]{2,0,1:T(8,128)S(1)} %get-tuple-element.32), channel_id=1, source_target_pairs={{1,0},{2,1},{3,2},{4,3},{5,4},{6,5},{7,6},{9,8},{10,9},{11,10},{12... | collective-permute-start | bytes 208904 | tf_op jit(solution)/shard_map/ppermute | solution.py:20
  215.8 3.6 %collective-permute-start.16 = (f32[1,32,512]{2,0,1:T(1,128)S(1)}, f32[1,32,512]{2,0,1:T(1,128)S(1)}, u32[]{:S(2)}, u32[]{:S(2)}) collective-permute-start(f32[1,32,512]{2,0,1:T(1,128)S(1)} %get-tuple-element.39), channel_id=1, source_target_pairs={{0,8},{8,16},{16,24},{1,9},{9,17},{17,25},{2,10},{10,18},{18,26},{... | collective-permute-start | bytes 196616 | tf_op jit(solution)/shard_map/ppermute | solution.py:18
  218.0 4.6 %collective-permute-start.17 = (f32[1,32,512]{2,0,1:T(1,128)S(1)}, f32[1,32,512]{2,0,1:T(1,128)S(1)}, u32[]{:S(2)}, u32[]{:S(2)}) collective-permute-start(f32[1,32,512]{2,0,1:T(1,128)S(1)} %get-tuple-element.40), channel_id=1, source_target_pairs={{8,0},{16,8},{24,16},{9,1},{17,9},{25,17},{10,2},{18,10},{26,18},{... | collective-permute-start | bytes 196616 | tf_op jit(solution)/shard_map/ppermute | solution.py:20
  223.4 9.1 %collective-permute-start.18 = (f32[34,1,512]{2,0,1:T(8,128)}, f32[34,1,512]{2,0,1:T(8,128)}, u32[]{:S(2)}, u32[]{:S(2)}) collective-permute-start(f32[34,1,512]{2,0,1:T(8,128)} %get-tuple-element.29), channel_id=1, source_target_pairs={{0,1},{1,2},{2,3},{3,4},{4,5},{5,6},{6,7},{8,9},{9,10},{10,11},{11... | collective-permute-start | bytes 208904 | tf_op jit(solution)/shard_map/ppermute | solution.py:18
  226.2 6.6 %collective-permute-start.19 = (f32[34,1,512]{2,0,1:T(8,128)}, f32[34,1,512]{2,0,1:T(8,128)}, u32[]{:S(2)}, u32[]{:S(2)}) collective-permute-start(f32[34,1,512]{2,0,1:T(8,128)} %get-tuple-element.30), channel_id=1, source_target_pairs={{1,0},{2,1},{3,2},{4,3},{5,4},{6,5},{7,6},{9,8},{10,9},{11,10},{12... | collective-permute-start | bytes 208904 | tf_op jit(solution)/shard_map/ppermute | solution.py:20
  (14 other events, 73.4 us)
